TPU v7x, 32 devices: a 4x4x1 block of a 4x4x8 slice. The times are simulated.
32 devices in a mesh: rep: 1 (over z), dp: 32 (over x, y, core).
Axes of the slice: x: 4, y: 4, z: 1, core: 2. Of those that a mesh axis runs over, the one named last changes fastest.
The devices are a block of a 4x4x8 slice.
Arguments:
- x: bfloat16 [32, 2048, 1024], P(('rep', 'dp'))
- dy: bfloat16 [32, 2048, 1024], P(('rep', 'dp'))
- w_gate: bfloat16 [2, 1024, 4096], replicated
- w_up: bfloat16 [2, 1024, 4096], replicated
- w_down: bfloat16 [2, 4096, 1024], replicated
- m_w_gate: float32 [2, 1024, 4096], P(None, 'dp')
- m_w_up: float32 [2, 1024, 4096], P(None, 'dp')
- m_w_down: float32 [2, 4096, 1024], P(None, 'dp')
- v_w_gate: float32 [2, 1024, 4096], P(None, 'dp')
- v_w_up: float32 [2, 1024, 4096], P(None, 'dp')
- v_w_down: float32 [2, 4096, 1024], P(None, 'dp')
Outputs:
- output 1: bfloat16 [2, 1024, 4096], P('rep')
- output 2: bfloat16 [2, 1024, 4096], P('rep')
- output 3: bfloat16 [2, 4096, 1024], P('rep')
- output 4: float32 [2, 1024, 4096], P('rep', 'dp')
- output 5: float32 [2, 1024, 4096], P('rep', 'dp')
- output 6: float32 [2, 4096, 1024], P('rep', 'dp')
- output 7: float32 [2, 1024, 4096], P('rep', 'dp')
- output 8: float32 [2, 1024, 4096], P('rep', 'dp')
- output 9: float32 [2, 4096, 1024], P('rep', 'dp')
All inputs are finite; a program needn't handle non-finite values.
Results may differ from a plain program's by a relative error of at most 0.022.
Values are sent between devices in bfloat16 or wider.
A program may use at most 768 MiB of HBM per device.

v0:
```python
import jax
import jax.numpy as jnp
from jax import lax

NAMES = ("w_gate", "w_up", "w_down")


def matmul(a, w):
    return jnp.dot(a, w, preferred_element_type=jnp.float32).astype(jnp.bfloat16)


def normed(h):
    wide = h.astype(jnp.float32)
    scale = lax.rsqrt(jnp.mean(wide**2, -1, keepdims=True) + 1e-6)
    return (wide * scale).astype(jnp.bfloat16)


def layer(h, w):
    a = normed(h)
    gate = jnp.dot(a, w["w_gate"], preferred_element_type=jnp.float32)
    up = jnp.dot(a, w["w_up"], preferred_element_type=jnp.float32)
    return h + matmul((jax.nn.silu(gate) * up).astype(jnp.bfloat16), w["w_down"])


def adamw(w, m, v, g):
    m = 0.9 * m + 0.1 * g
    v = 0.95 * v + 0.05 * g * g
    step = m * lax.rsqrt(v + 1e-8) + 0.1 * w
    return (w - 0.02 * step).astype(jnp.bfloat16), m, v


def stack(weights, h):
    for number in range(weights["w_gate"].shape[0]):
        h = layer(h, {name: w[number] for name, w in weights.items()})
    return h


def solution(mesh):
    groups = mesh.shape["rep"]

    def step(x, dy, *arrays):
        weights, m, v = (arrays[i : i + 3] for i in (0, 3, 6))
        x, dy = (t.reshape(groups, -1, *t.shape[1:]) for t in (x, dy))

        def of_a_group(x, dy):
            _, back = jax.vjp(lambda w: stack(w, x), dict(zip(NAMES, weights, strict=True)))
            by_weights = back(dy)[0]
            gradients = [by_weights[name].astype(jnp.float32) for name in NAMES]
            new = [adamw(w.astype(jnp.float32), m, v, g) for w, m, v, g in zip(weights, m, v, gradients, strict=True)]
            return tuple(one[which] for which in range(3) for one in new)

        return tuple(t.reshape(-1, *t.shape[2:]) for t in jax.vmap(of_a_group)(x, dy))

    return step
```

profile of v0, /device:TPU:97, one launch (start us, length us, event | category | flops | bytes accessed | tf_op | source)
XLA Modules:
  0.0 1145.0 jit_solution(17433879085332765799)
XLA Ops:
  16.8 24.5 %fusion.54 = f32[2048,4096]{1,0:T(8,128)} fusion(bf16[2,1024,4096]{2,1,0:T(8,128)(2,1)} %param, bf16[1,2048,1024]{2,1,0:T(8,128)(2,1)} %param.4, f32[2048]{0:T(1024)S(1)} %add_rsqrt_fusion), kind=kOutput, calls=%fused_computation.71 | convolution fusion | flops 17186160640 | bytes 46145536 | tf_op jit(solution)/vmap(jvp())/dot_general | solution.py:20
  41.3 23.3 %fusion.52 = f32[2048,4096]{1,0:T(8,128)} fusion(bf16[2,1024,4096]{2,1,0:T(8,128)(2,1)} %param.5, bf16[1,2048,1024]{2,1,0:T(8,128)(2,1)S(1)} %copy-done.2, f32[2048]{0:T(1024)S(1)} %add_rsqrt_fusion), kind=kOutput, calls=%fused_computation.69 | convolution fusion | flops 17186160640 | bytes 46145536 | tf_op jit(solution)/vmap(jvp())/dot_general | solution.py:21
  64.7 27.5 %fusion.26 = bf16[2048,4096]{1,0:T(8,128)(2,1)} fusion(f32[2048,4096]{1,0:T(8,128)} %fusion.52, f32[2048,4096]{1,0:T(8,128)} %fusion.54), kind=kLoop, calls=%fused_computation.35 | loop fusion | flops 50331648 | bytes 83886080
  92.2 24.0 %fusion.39 = (f32[2048]{0:T(1024)S(1)}, bf16[1,2048,1024]{1,2,0:T(8,128)(2,1)S(1)}) fusion(bf16[1,2048,1024]{1,2,0:T(8,128)(2,1)} %copy, bf16[2048,4096]{1,0:T(8,128)(2,1)} %fusion.26, bf16[2,4096,1024]{2,1,0:T(8,128)(2,1)} %param.3), kind=kOutput, calls=%fused_computation.56 | convolution fusion | flops 17190352896 | bytes 33562624 | tf_op jit(solution)/vmap(jvp())/dot_general | solution.py:9
  116.9 24.1 %fusion.42 = f32[2048,4096]{1,0:T(8,128)} fusion(bf16[2,1024,4096]{2,1,0:T(8,128)(2,1)} %param, bf16[1,2048,1024]{1,2,0:T(8,128)(2,1)S(1)} %get-tuple-element.10, f32[2048]{0:T(1024)S(1)} %bitcast.312), kind=kOutput, calls=%fused_computation.59 | convolution fusion | flops 17186160640 | bytes 46145536 | tf_op jit(solution)/vmap(jvp())/dot_general | solution.py:20
  141.0 23.5 %fusion.46 = f32[2048,4096]{1,0:T(8,128)} fusion(bf16[2,1024,4096]{2,1,0:T(8,128)(2,1)} %param.5, bf16[1,2048,1024]{1,2,0:T(8,128)(2,1)S(1)} %get-tuple-element.10, f32[2048]{0:T(1024)S(1)} %bitcast.313), kind=kOutput, calls=%fused_computation.63 | convolution fusion | flops 17186160640 | bytes 46145536 | tf_op jit(solution)/vmap(jvp())/dot_general | solution.py:21
  164.4 32.1 %fusion.28 = f32[4096,1024]{1,0:T(8,128)} fusion(f32[2048,4096]{1,0:T(8,128)} %fusion.46, f32[2048,4096]{1,0:T(8,128)} %fusion.42, bf16[1,2048,1024]{2,1,0:T(8,128)(2,1)} %param.2), kind=kOutput, calls=%fused_computation.37 | convolution fusion | flops 17230200832 | bytes 88080384 | tf_op jit(solution)/vmap(transpose(jvp()))/dot_general | solution.py:9
  203.5 24.4 %convolution_convert_fusion.1 = bf16[2048,4096]{1,0:T(8,128)(2,1)} fusion(bf16[2,4096,1024]{2,1,0:T(8,128)(2,1)} %param.3, bf16[1,2048,1024]{2,1,0:T(8,128)(2,1)} %param.2), kind=kOutput, calls=%fused_computation.44 | convolution fusion | flops 17188257792 | bytes 29360128 | tf_op jit(solution)/vmap(transpose(jvp()))/dot_general | solution.py:9
  227.8 32.9 %fusion.6 = bf16[2048,4096]{1,0:T(8,128)(2,1)} fusion(f32[2048,4096]{1,0:T(8,128)} %fusion.42, f32[2048,4096]{1,0:T(8,128)} %fusion.46, bf16[2048,4096]{1,0:T(8,128)(2,1)} %convolution_convert_fusion.1), kind=kLoop, calls=%fused_computation.11 | loop fusion | flops 100663296 | bytes 100663296
  260.8 27.0 %fusion.24 = bf16[2048,1024]{0,1:T(8,128)(2,1)} fusion(bf16[2048,4096]{1,0:T(8,128)(2,1)} %convolution_convert_fusion.1, f32[2048,4096]{1,0:T(8,128)} %fusion.42, bf16[2,1024,4096]{2,1,0:T(8,128)(2,1)} %param.5), kind=kOutput, calls=%fused_computation.34 | convolution fusion | flops 17230200832 | bytes 62914560 | tf_op jit(solution)/vmap(transpose(jvp()))/dot_general | solution.py:21
  287.7 25.0 %fusion.41 = (f32[2048]{0:T(1024)S(1)}, bf16[2048,1024]{0,1:T(8,128)(2,1)S(1)}) fusion(bf16[1,2048,1024]{1,2,0:T(8,128)(2,1)} %copy-done.3, bf16[2048,1024]{0,1:T(8,128)(2,1)} %fusion.24, bf16[2048,4096]{1,0:T(8,128)(2,1)} %fusion.6, bf16[2,1024,4096]{2,1,0:T(8,128)(2,1)} %param), kind=kOutput, calls=%fused_computation.58 | convolution fusion | flops 17190352896 | bytes 37756928 | tf_op jit(solution)/vmap(transpose(jvp()))/dot_general | solution.py:20
  318.0 23.0 %fusion.117 = f32[1024,4096]{0,1:T(8,128)} fusion(bf16[2048,1024]{0,1:T(8,128)(2,1)S(1)} %fusion.68, bf16[2048,4096]{1,0:T(8,128)(2,1)} %fusion.26), kind=kOutput, calls=%fused_computation.148 | convolution fusion | flops 17179869184 | bytes 37748736 | tf_op jit(solution)/vmap(transpose(jvp()))/dot_general | solution.py:9
  341.1 23.8 %fusion.77 = f32[4096,1024]{0,1:T(8,128)} fusion(bf16[2048,4096]{1,0:T(8,128)(2,1)} %fusion.6, bf16[1,2048,1024]{1,2,0:T(8,128)(2,1)} %copy-done.3, f32[2048]{0:T(1024)S(1)} %bitcast.315), kind=kOutput, calls=%fused_computation.91 | convolution fusion | flops 17186160640 | bytes 37756928 | tf_op jit(solution)/vmap(transpose(jvp()))/dot_general | solution.py:20
  365.1 24.8 %convolution_convert_fusion = bf16[2048,4096]{1,0:T(8,128)(2,1)} fusion(bf16[2048,1024]{0,1:T(8,128)(2,1)} %copy-done.5, bf16[2,4096,1024]{2,1,0:T(8,128)(2,1)} %param.3), kind=kOutput, calls=%fused_computation.43 | convolution fusion | flops 17188257792 | bytes 29360128 | tf_op jit(solution)/vmap(transpose(jvp()))/dot_general | solution.py:9
  389.9 39.4 %fusion.10 = f32[4096,1024]{0,1:T(8,128)} fusion(f32[2048,4096]{1,0:T(8,128)} %fusion.54, f32[2048,4096]{1,0:T(8,128)} %fusion.52, bf16[2048,4096]{1,0:T(8,128)(2,1)} %convolution_convert_fusion, bf16[1,2048,1024]{2,1,0:T(8,128)(2,1)} %param.4, f32[2048]{0:T(1024)S(1)} %copy-done.14), kind=kOutput, calls=%fused_computation.15 | convolution fusion | flops 17278435328 | bytes 104865792 | tf_op jit(solution)/vmap(transpose(jvp()))/dot_general | solution.py:20
  429.4 29.4 %fusion.22 = f32[4096,1024]{0,1:T(8,128)} fusion(bf16[2048,4096]{1,0:T(8,128)(2,1)} %convolution_convert_fusion.1, f32[2048,4096]{1,0:T(8,128)} %fusion.42, bf16[1,2048,1024]{1,2,0:T(8,128)(2,1)} %copy-done.3, f32[2048]{0:T(1024)S(1)} %bitcast.316), kind=kOutput, calls=%fused_computation.33 | convolution fusion | flops 17236492288 | bytes 71311360 | tf_op jit(solution)/vmap(transpose(jvp()))/dot_general | solution.py:21
  459.0 29.7 %fusion.2 = f32[4096,1024]{0,1:T(8,128)} fusion(bf16[2048,4096]{1,0:T(8,128)(2,1)} %convolution_convert_fusion, f32[2048,4096]{1,0:T(8,128)} %fusion.54, bf16[1,2048,1024]{2,1,0:T(8,128)(2,1)} %param.4, f32[2048]{0:T(1024)S(1)} %copy-done.14), kind=kOutput, calls=%fused_computation.8 | convolution fusion | flops 17236492288 | bytes 71311360 | tf_op jit(solution)/vmap(transpose(jvp()))/dot_general | solution.py:21
  494.5 67.1 %reduce-scatter.19.cloned.1.call-done = f32[4096,32]{0,1:T(8,128)} async-done(((f32[4096,1024]{0,1:T(8,128)}), f32[4096,32]{0,1:T(8,128)}) %reduce-scatter.19.cloned.1.call-update) | async-done | bytes 524304
  562.7 110.0 %reduce-scatter.21.cloned.1.call-done = f32[4096,32]{0,1:T(8,128)} async-done(((f32[4096,1024]{0,1:T(8,128)}), f32[4096,32]{0,1:T(8,128)}) %reduce-scatter.21.cloned.1.call-update) | async-done | bytes 524304
  677.3 105.8 %reduce-scatter.23.cloned.1.call-done = f32[4096,32]{0,1:T(8,128)} async-done(((f32[4096,1024]{0,1:T(8,128)}), f32[4096,32]{0,1:T(8,128)}) %reduce-scatter.23.cloned.1.call-update) | async-done | bytes 524304
  784.2 109.9 %reduce-scatter.25.cloned.1.call-done = f32[4096,32]{0,1:T(8,128)} async-done(((f32[4096,1024]{0,1:T(8,128)}), f32[4096,32]{0,1:T(8,128)}) %reduce-scatter.25.cloned.1.call-update) | async-done | bytes 524304
  899.0 66.0 %all-gather.14.cloned.1.call-done = bf16[1,2,4096,1024]{3,2,1,0:T(8,128)(2,1)} async-done(((bf16[1,2,128,1024]{3,2,1,0:T(8,128)(2,1)}), bf16[1,2,4096,1024]{3,2,1,0:T(8,128)(2,1)}) %all-gather.14.cloned.1.call-update) | async-done | bytes 16777232 | tf_op jit(solution)/reshape | solution.py:52
  965.0 69.4 %all-gather.10.cloned.1.call-done = bf16[1,2,1024,4096]{3,2,1,0:T(8,128)(2,1)} async-done(((bf16[1,2,32,4096]{3,2,1,0:T(8,128)(2,1)}), bf16[1,2,1024,4096]{3,2,1,0:T(8,128)(2,1)}) %all-gather.10.cloned.1.call-update) | async-done | bytes 16777232 | tf_op jit(solution)/reshape | solution.py:52
  1034.4 69.5 %all-gather.12.cloned.1.call-done = bf16[1,2,1024,4096]{3,2,1,0:T(8,128)(2,1)} async-done(((bf16[1,2,32,4096]{3,2,1,0:T(8,128)(2,1)}), bf16[1,2,1024,4096]{3,2,1,0:T(8,128)(2,1)}) %all-gather.12.cloned.1.call-update) | async-done | bytes 16777232 | tf_op jit(solution)/reshape | solution.py:52
  (79 shorter events, 74.2 us)
Async XLA Ops:
  7.2 481.7 %reduce-scatter.27.cloned.1.call-start = ((), (), s32[]{:S(2)}) async-start(), calls=%async_computation.13 | async-start | bytes 17301504
  16.8 24.6 %copy-start.13 = (f32[2048]{0:T(1024)}, f32[2048]{0:T(1024)S(1)}, u32[]{:S(2)}) copy-start(f32[2048]{0:T(1024)S(1)} %add_rsqrt_fusion) | copy-start | bytes 24580
  16.8 24.6 %copy-start.2 = (bf16[1,2048,1024]{2,1,0:T(8,128)(2,1)S(1)}, bf16[1,2048,1024]{2,1,0:T(8,128)(2,1)}, u32[]{:S(2)}) copy-start(bf16[1,2048,1024]{2,1,0:T(8,128)(2,1)} %param.4) | copy-start | bytes 12582916
  116.2 24.8 %copy-start.3 = (bf16[1,2048,1024]{1,2,0:T(8,128)(2,1)}, bf16[1,2048,1024]{1,2,0:T(8,128)(2,1)S(1)}, u32[]{:S(2)}) copy-start(bf16[1,2048,1024]{1,2,0:T(8,128)(2,1)S(1)} %get-tuple-element.10) | copy-start | bytes 12582916
  116.9 24.1 %copy-start.11 = (f32[1,2048]{1,0:T(1,128)}, f32[1,2048]{1,0:T(1,128)S(1)}, u32[]{:S(2)}) copy-start(f32[1,2048]{1,0:T(1,128)S(1)} %rsqrt.29) | copy-start | bytes 24580
  196.6 293.5 %reduce-scatter.29.cloned.1.call-start = ((), (), s32[]{:S(2)}) async-start(), calls=%async_computation.14 | async-start | bytes 17301504
  287.7 25.0 %copy-start.10 = (f32[2048]{0:T(1024)S(1)}, f32[2048]{0:T(1024)}, u32[]{:S(2)}) copy-start(f32[2048]{0:T(1024)} %copy-done.9) | copy-start | bytes 24580
  287.7 25.1 %copy-start = (bf16[1,2048,1024]{1,2,0:T(8,128)(2,1)S(1)}, bf16[1,2048,1024]{1,2,0:T(8,128)(2,1)}, u32[]{:S(2)}) copy-start(bf16[1,2048,1024]{1,2,0:T(8,128)(2,1)} %copy.1) | copy-start | bytes 12582916
  287.7 25.1 %copy-start.4 = (bf16[1,2048,1024]{1,2,0:T(8,128)(2,1)S(1)}, bf16[1,2048,1024]{1,2,0:T(8,128)(2,1)}, u32[]{:S(2)}) copy-start(bf16[1,2048,1024]{1,2,0:T(8,128)(2,1)} %copy-done.3) | copy-start | bytes 12582916
  287.7 25.1 %copy-start.12 = (f32[1,2048]{1,0:T(1,128)S(1)}, f32[1,2048]{1,0:T(1,128)}, u32[]{:S(2)}) copy-start(f32[1,2048]{1,0:T(1,128)} %copy-done.11) | copy-start | bytes 24580
  341.1 220.5 %reduce-scatter.19.cloned.1.call-start = ((), (), s32[]{:S(2)}) async-start(), calls=%async_computation.9 | async-start | bytes 17301504
  365.0 24.9 %copy-start.14 = (f32[2048]{0:T(1024)S(1)}, f32[2048]{0:T(1024)}, u32[]{:S(2)}) copy-start(f32[2048]{0:T(1024)} %copy-done.13) | copy-start | bytes 24580
  365.0 307.7 %reduce-scatter.21.cloned.1.call-start = ((), (), s32[]{:S(2)}) async-start(), calls=%async_computation.10 | async-start | bytes 17301504
  429.4 353.8 %reduce-scatter.23.cloned.1.call-start = ((), (), s32[]{:S(2)}) async-start(), calls=%async_computation.11 | async-start | bytes 17301504
  458.9 435.2 %reduce-scatter.25.cloned.1.call-start = ((), (), s32[]{:S(2)}) async-start(), calls=%async_computation.12 | async-start | bytes 17301504
  488.7 185.1 %copy-start.8 = (f32[2,32,4096]{2,1,0:T(8,128)S(1)}, f32[2,32,4096]{2,1,0:T(8,128)}, u32[]{:S(2)}) copy-start(f32[2,32,4096]{2,1,0:T(8,128)} %param.6) | copy-start | bytes 3145732
  488.8 476.2 %all-gather.14.cloned.1.call-start = ((), (), s32[]{:S(2)}) async-start(), calls=%async_computation.8 | async-start | bytes 17301504 | tf_op jit(solution)/reshape | solution.py:52
  494.4 540.0 %all-gather.10.cloned.1.call-start = ((), (), s32[]{:S(2)}) async-start(), calls=%async_computation.6 | async-start | bytes 17301504 | tf_op jit(solution)/reshape | solution.py:52
  677.3 426.6 %all-gather.12.cloned.1.call-start = ((), (), s32[]{:S(2)}) async-start(), calls=%async_computation.7 | async-start | bytes 17301504 | tf_op jit(solution)/reshape | solution.py:52
  1103.9 16.8 %copy-start.1 = (bf16[1,2,1024,4096]{3,2,1,0:T(8,128)(2,1)S(1)}, bf16[1,2,1024,4096]{3,2,1,0:T(8,128)(2,1)}, u32[]{:S(2)}) copy-start(bf16[1,2,1024,4096]{3,2,1,0:T(8,128)(2,1)} %all-gather.12.cloned.1.call-done) | copy-start | bytes 50331652
  1103.9 25.3 %slice-start = ((s8[16777216]{0:T(1024)(128)(4,1)}), s8[4194304]{0:T(1024)(128)(4,1)S(1)}, s32[]{:S(2)}) async-start(s8[16777216]{0:T(1024)(128)(4,1)} %bitcast.304), calls=%async_computation.15 | async-start | bytes 8388608
  1103.9 25.3 %slice-start.1 = ((s8[16777216]{0:T(1024)(128)(4,1)}), s8[4194304]{0:T(1024)(128)(4,1)S(1)}, s32[]{:S(2)}) async-start(s8[16777216]{0:T(1024)(128)(4,1)} %bitcast.304), calls=%async_computation.16 | async-start | bytes 8388608
  1120.7 9.9 slice-start.2
  1120.7 11.1 slice-start.3
  (4 other events, 7.7 us)
Sparse Core Ops, SparseCore 0:
  196.8 109.7 reduce-scatter.26
  341.2 109.7 reduce-scatter.28
  454.7 106.8 reduce-scatter.18
  565.8 106.8 reduce-scatter.20
  676.3 106.8 reduce-scatter.22
  787.3 106.7 reduce-scatter.24
  896.3 68.6 all-gather.13
  967.7 66.6 all-gather.9
  1037.2 66.6 all-gather.11
where the time goes:
time: 1150 us; the launch traced here: 1140 us
  waiting for transfers between devices  598 us (52%)
  matrix products  398 us (35%)
  other arithmetic  83.5 us (7%)
  local copies, waits for them, and re-layouts  50 us (4%)
  between operations  14.6 us (1%)
    unnamed x15, waiting for transfers between devices  393 us
    reshape x3, waiting for transfers between devices, step(): t.reshape(-1, *t.shape[2:])  205 us
    dot_general x5, matrix products, layer(): gate = jnp.dot(a, w['w_gate'], preferred_element_type=jnp.float32)  137 us
    dot_general x5, matrix products, layer(): up = jnp.dot(a, w['w_up'], preferred_element_type=jnp.float32)  133 us
    dot_general x5, matrix products, matmul(): jnp.dot(a, w, preferred_element_type=jnp.float32).astype(jnp.bfloat16)  128 us
    unnamed x4, other arithmetic  63.6 us
    unnamed x43, local copies, waits for them, and re-layouts  50 us
  transfers between devices with their start and end apart: 9, of which 7 were waited for; matrix products, arithmetic and copies ran while one was open for 27% of the time, Pallas kernels for 0%

commit v1 on v0

v1 whole, which is shorter than its diff:
```python
import functools
import jax, jax.numpy as jnp
from jax import lax
from jax.experimental import pallas as pl
from jax.experimental.pallas import tpu as pltpu
bf=jnp.bfloat16; f32=jnp.float32
VM=62*2**20
def dot(a,b): return jnp.dot(a,b,preferred_element_type=f32)
def dot_nt(a,b): return lax.dot_general(a,b,(((1,),(1,)),((),())),preferred_element_type=f32)
def normed(h):
    wide=h.astype(f32)
    return (wide*lax.rsqrt(jnp.mean(wide**2,-1,keepdims=True)+1e-6)).astype(bf)

def p0(x,wg,wu,tm=1024,tf=512,rm=256,rf=256):
    T,Dm=x.shape; F=wg.shape[-1]
    def kern(x_ref,wg_ref,wu_ref,hid_ref,hidT_ref,s_ref,t_ref,aT_ref,a_sc):
        f=pl.program_id(0); t=pl.program_id(1)
        @pl.when(f==0)
        def _():
            a=normed(x_ref[...])
            a_sc[pl.ds(pl.multiple_of(t*tm,tm),tm),:]=a
            aT_ref[...]=a.T
        for r in range(tm//rm):
            a=a_sc[pl.ds(pl.multiple_of(t*tm+r*rm,rm),rm),:]
            for c in range(tf//rf):
                cs=slice(c*rf,(c+1)*rf); rs=slice(r*rm,(r+1)*rm)
                gate=dot(a,wg_ref[0,:,cs]); up=dot(a,wu_ref[0,:,cs])
                sg=jax.nn.sigmoid(gate); s=gate*sg
                s_ref[rs,cs]=s
                t_ref[rs,cs]=up*(sg*(1.0+gate*(1.0-sg)))
                hid=(s*up).astype(bf)
                hid_ref[rs,cs]=hid
                hidT_ref[cs,rs]=hid.T
    nt=T//tm; last=nt-1
    return pl.pallas_call(kern,grid=(F//tf,nt),
        in_specs=[pl.BlockSpec((tm,Dm),lambda f,t:(jnp.where(f==0,t,last),0)),
                  pl.BlockSpec((1,Dm,tf),lambda f,t:(0,0,f)),pl.BlockSpec((1,Dm,tf),lambda f,t:(0,0,f))],
        out_specs=[pl.BlockSpec((tm,tf),lambda f,t:(t,f)),pl.BlockSpec((tf,tm),lambda f,t:(f,t)),
                   pl.BlockSpec((tm,tf),lambda f,t:(t,f)),pl.BlockSpec((tm,tf),lambda f,t:(t,f)),
                   pl.BlockSpec((Dm,tm),lambda f,t:(0,jnp.where(f==0,t,last)))],
        out_shape=[jax.ShapeDtypeStruct((T,F),bf),jax.ShapeDtypeStruct((F,T),bf),jax.ShapeDtypeStruct((T,F),f32),jax.ShapeDtypeStruct((T,F),f32),jax.ShapeDtypeStruct((Dm,T),bf)],
        scratch_shapes=[pltpu.VMEM((T,Dm),bf)],
        compiler_params=pltpu.CompilerParams(vmem_limit_bytes=VM,dimension_semantics=("arbitrary","arbitrary")),name="p0")(x,wg,wu)

def p1(x,hid,wd,tm=512):
    T,Dm=x.shape; F=hid.shape[1]
    def kern(x_ref,hid_ref,wd_ref,h_ref,a_ref,aT_ref):
        for r in range(tm//256):
            rs=slice(r*256,(r+1)*256)
            y=dot(hid_ref[rs,:],wd_ref[0]).astype(bf)
            h=x_ref[rs,:]+y
            h_ref[rs,:]=h
            a=normed(h)
            a_ref[rs,:]=a
            aT_ref[:,rs]=a.T
    return pl.pallas_call(kern,grid=(T//tm,),
        in_specs=[pl.BlockSpec((tm,Dm),lambda t:(t,0)),pl.BlockSpec((tm,F),lambda t:(t,0)),pl.BlockSpec((1,F,Dm),lambda t:(0,0,0))],
        out_specs=[pl.BlockSpec((tm,Dm),lambda t:(t,0)),pl.BlockSpec((tm,Dm),lambda t:(t,0)),pl.BlockSpec((Dm,tm),lambda t:(0,t))],
        out_shape=[jax.ShapeDtypeStruct((T,Dm),bf),jax.ShapeDtypeStruct((T,Dm),bf),jax.ShapeDtypeStruct((Dm,T),bf)],
        compiler_params=pltpu.CompilerParams(vmem_limit_bytes=VM),name="p1")(x,hid,wd)

def p2(a,dy,wg,wu,wd,layer,tm=1024,tf=512,rm=256,rf=256):
    T,Dm=a.shape; F=wg.shape[-1]
    def kern(a_ref,dy_ref,wg_ref,wu_ref,wd_ref,hidT_ref,dg_ref,du_ref):
        t=pl.program_id(1)
        for r in range(tm//rm):
            ro=pl.ds(pl.multiple_of(t*tm+r*rm,rm),rm)
            av=a_ref[ro,:]; dv=dy_ref[ro,:]
            for c in range(tf//rf):
                cs=slice(c*rf,(c+1)*rf); rs=slice(r*rm,(r+1)*rm)
                gate=dot(av,wg_ref[0,:,cs]); up=dot(av,wu_ref[0,:,cs])
                dh=dot_nt(dv,wd_ref[0,cs,:]).astype(bf).astype(f32)
                sg=jax.nn.sigmoid(gate); s=gate*sg
                du_ref[rs,cs]=(dh*s).astype(bf)
                dg_ref[rs,cs]=(dh*(up*(sg*(1.0+gate*(1.0-sg))))).astype(bf)
                hidT_ref[cs,rs]=(s*up).astype(bf).T
    return pl.pallas_call(kern,grid=(F//tf,T//tm),
        in_specs=[pl.BlockSpec((T,Dm),lambda f,t:(0,0)),pl.BlockSpec((T,Dm),lambda f,t:(0,0)),
                  pl.BlockSpec((1,Dm,tf),lambda f,t:(layer,0,f)),pl.BlockSpec((1,Dm,tf),lambda f,t:(layer,0,f)),pl.BlockSpec((1,tf,Dm),lambda f,t:(layer,f,0))],
        out_specs=[pl.BlockSpec((tf,tm),lambda f,t:(f,t)),pl.BlockSpec((tm,tf),lambda f,t:(t,f)),pl.BlockSpec((tm,tf),lambda f,t:(t,f))],
        out_shape=[jax.ShapeDtypeStruct((F,T),bf),jax.ShapeDtypeStruct((T,F),bf),jax.ShapeDtypeStruct((T,F),bf)],
        compiler_params=pltpu.CompilerParams(vmem_limit_bytes=VM),name="p2")(a,dy,wg,wu,wd)
import math
MESH=pl.DeviceIdType.MESH
div,rem=lax.div,lax.rem

def mega(n,hid1T,a1T,hid0T,a0T,dy,dg1,du1,wg,wu,wd,s0,t0,h1,mg,mu,md,vg,vu,vd,axis="dp"):
    T,Dm=dy.shape; L,_,F=wg.shape
    S=math.isqrt(n//2); R=Dm//n; Q=Dm//4; K=F//Dm
    assert S==4 and 2*S*S==n and F==4*Dm and L==2 and R%16==0 and Q%128==0
    U=3*L*K; N=U+8; TM=T//4
    hv=lambda h: h.reshape(S,S,2,K,R,T)
    av=lambda a: a.reshape(S,S,2,R,T)
    def kern(hid1T,a1T,hid0T,a0T,dy,dg1,du1,wg,wu,wd,s0,t0,h1,mg,mu,md,vg,vu,vd,
             wag,gsum,dg0,du0,
             lhs,rhs,own,dsend,drecv,r1,r2,r3,e1,e2,e3,pf,q1,q2,q3,x1,x2,x3,wst,win,min_,vin,gst,
             wbuf,gt,ut,ht,yt,st,tt,
             lsem,rsem,wsem,gsem,ssem,osem,isem,nsem,csem,
             dss,drs,ss,rs,ads,adr):
        me=lax.axis_index(axis)
        c=rem(me,2); y=rem(div(me,2),S); x=div(me,2*S)
        idx=lambda x,y,c: (rem(x+S,S)*S+rem(y+S,S))*2+c
        nb=[idx(x+1,y,c),idx(x-1,y,c),idx(x,y+1,c),idx(x,y-1,c)]; pa=idx(x,y,1-c)
        bar=pltpu.get_barrier_semaphore()
        for d in nb+[pa]:
            pl.semaphore_signal(bar,inc=1,device_id={axis:d},device_id_type=MESH)
        pl.semaphore_wait(bar,5)
        AB=[(x,y),(y,x)]
        P1=[(0,1),(2,3)]; P2=[(2,3),(0,1)]
        def rc(src,dst,s,r,dev):
            return pltpu.make_async_remote_copy(src_ref=src,dst_ref=dst,send_sem=s,recv_sem=r,device_id={axis:dev},device_id_type=MESH)
        cp=pltpu.make_async_copy
        def jk(u):
            l,v=div(u,3*K),rem(u,3*K); w=v-K
            return 3*l+jnp.where(v<K,0,1+rem(w,2)),jnp.where(v<K,v,div(w,2))
        def loc(u): j,k=jk(u); return j*K+k
        two=lambda u: rem(u,2)
        four=lambda u: rem(u,4)
        def sems(kind,u,d): return ss.at[kind,two(u),d],rs.at[kind,four(u),d],nb[d]
        m1,m2,m3,o1,o2,o3=(lambda u,d,kind=kind,e=e,r=r: rc(e.at[two(u),d],r.at[four(u),d],*sems(kind,u,d))
                           for kind,(e,r) in enumerate(((e1,r1),(e2,r2),(e3,r3),(x1,q1),(x2,q2),(x3,q3))))
        pair=lambda g: pl.ds(2*g,2)
        up_,down_=(lambda v: rem(v+1,S)),(lambda v: rem(v+S-1,S))
        behind=lambda v,s: (down_,up_)[s](v)
        far_=lambda v: rem(v+2,S)
        def g1(u,g,s):
            a,b=AB[g]; d=P2[g][s]
            return rc(wst.at[two(u),pair(g)],wag.at[loc(u),c,pair(g),a,b],*sems(6,u,d))
        def g2(u,g,s):
            a,b=AB[g]; d=P2[g][s]; r=wag.at[loc(u),c,2*g+s,a,behind(b,s)]
            return rc(r,r,*sems(7,u,d))
        def g3(u,g,s):
            a,b=AB[g]; d=P1[g][s]; r=wag.at[loc(u),c,pair(g),a]
            return rc(r,r,*sems(8,u,d))
        def g4(u,g,s):
            a,b=AB[g]; d=P1[g][s]; r=wag.at[loc(u),c,2*g+s,behind(a,s)]
            return rc(r,r,*sems(9,u,d))
        def d2(u): return rc(dsend,drecv.at[four(u)],dss,drs.at[four(u)],pa)
        def gd(u): return rc(wag.at[loc(u),c],wag.at[loc(u),c],ads.at[two(u)],adr.at[four(u)],pa)
        GS=[(g,s) for g in range(2) for s in range(2)]
        f=lambda v: v.astype(f32)
        def lhs_load(u,h):
            j,k=jk(u); cc=(1-c) if h else c; dst=lhs.at[h]; sem=lsem.at[h]
            @pl.when(j==0)
            def _(): cp(hid1T.at[:,:,cc,k],dst,sem).start()
            @pl.when(u==K)
            def _(): cp(a1T.at[:,:,cc],dst,sem).start()
            @pl.when(j==3)
            def _(): cp(hid0T.at[:,:,cc,k],dst,sem).start()
            @pl.when(u==4*K)
            def _(): cp(a0T.at[:,:,cc],dst,sem).start()
        def lhs_wait(u,h):
            @pl.when(rem(u,3*K)<=K)
            def _(): cp(a1T.at[:,:,c],lhs.at[h],lsem.at[h]).wait()
        def rhs_load(u):
            j,k=jk(u); dst=rhs.at[0]; sem=rsem; cols=pl.ds(pl.multiple_of(k*Dm,Dm),Dm)
            @pl.when(u==0)
            def _(): cp(dy,dst,sem).start()
            @pl.when(j==1)
            def _(): cp(dg1.at[:,cols],dst,sem).start()
            @pl.when(j==2)
            def _(): cp(du1.at[:,cols],dst,sem).start()
            @pl.when(j==4)
            def _(): cp(dg0.at[:,cols],dst,sem).start()
            @pl.when(j==5)
            def _(): cp(du0.at[:,cols],dst,sem).start()
        def rhs_wait(u):
            @pl.when((u==0)|(rem(u,3*K)>=K))
            def _(): cp(dy,rhs.at[0],rsem).wait()
        def state(u,go):
            j,k=jk(u); l=1-div(j,3); t=rem(j,3); sl=two(u)
            cols=pl.ds(pl.multiple_of(k*Dm,Dm),Dm)
            def three(mr,vr,wr):
                go(cp(mr,min_.at[sl],isem.at[0,sl])); go(cp(vr,vin.at[sl],isem.at[1,sl])); go(cp(wr,win.at[sl],isem.at[2,sl]))
            @pl.when(t==0)
            def _():
                r=pl.ds(pl.multiple_of(k*R,R),R)
                three(md.at[l,r],vd.at[l,r],wd.at[l,pl.ds(pl.multiple_of(me*(K*R)+k*R,R),R)])
            @pl.when(t==1)
            def _(): three(mg.at[l,:,cols],vg.at[l,:,cols],wg.at[l,pl.ds(pl.multiple_of(me*R,R),R),cols])
            @pl.when(t==2)
            def _(): three(mu.at[l,:,cols],vu.at[l,:,cols],wu.at[l,pl.ds(pl.multiple_of(me*R,R),R),cols])
        start=lambda d: d.start()
        wait=lambda d: d.wait()
        def both(q,o,u): return f(own[rem(u,3),q,o])+f(drecv[four(u),q,o])
        def at(i,dl,body):
            u=i-dl
            @pl.when((u>=0)&(u<U))
            def _(): body(u)
        def sA1(u):
            d2(u).wait()
            sl=four(u); w=two(u)
            for g in range(2):
                a,b=AB[g]; p,m=P1[g]
                far=far_(a)
                e1[w,p]=both(2*g,far,u).astype(bf); m1(u,p).start()
                e1[w,m]=both(2*g+1,far,u).astype(bf); m1(u,m).start()
            for g in range(2):
                a,b=AB[g]; p,m=P1[g]
                e2[w,p]=both(2*g+1,up_(a),u).astype(bf); m2(u,p).start()
                e2[w,m]=both(2*g,down_(a),u).astype(bf); m2(u,m).start()
        def sA2(u):
            sl=four(u); w=two(u)
            for d in range(4): m1(u,d).wait_send(); m2(u,d).wait_send()
            for g in range(2):
                a,b=AB[g]; p,m=P1[g]
                m1(u,p).wait_recv()
                e3[w,p]=(both(2*g,up_(a),u)+f(r1[sl,p])).astype(bf); m3(u,p).start()
                m1(u,m).wait_recv()
                e3[w,m]=(both(2*g+1,down_(a),u)+f(r1[sl,m])).astype(bf); m3(u,m).start()
        def sA3(u):
            sl=four(u); w=two(u)
            for d in range(4): m3(u,d).wait_send()
            for g in range(2):
                a,b=AB[g]; p,m=P1[g]
                for d in (p,m): m2(u,d).wait_recv(); m3(u,d).wait_recv()
                pf[w,2*g]=both(2*g,a,u)+f(r3[sl,p])+f(r2[sl,m])
                pf[w,2*g+1]=both(2*g+1,a,u)+f(r2[sl,p])+f(r3[sl,m])
                p,m=P2[g]; far=far_(b)
                x1[w,p]=pf[w,2*g,far].astype(bf); o1(u,p).start()
                x1[w,m]=pf[w,2*g+1,far].astype(bf); o1(u,m).start()
                x2[w,p]=pf[w,2*g+1,up_(b)].astype(bf); o2(u,p).start()
                x2[w,m]=pf[w,2*g,down_(b)].astype(bf); o2(u,m).start()
        def sB3(u):
            sl=four(u); w=two(u)
            for g in range(2):
                a,b=AB[g]; p,m=P2[g]
                o1(u,p).wait_recv()
                x3[w,p]=(pf[w,2*g,up_(b)]+f(q1[sl,p])).astype(bf); o3(u,p).start()
                o1(u,m).wait_recv()
                x3[w,m]=(pf[w,2*g+1,down_(b)]+f(q1[sl,m])).astype(bf); o3(u,m).start()
            for d in range(4): o1(u,d).wait_send(); o2(u,d).wait_send()
        def sA4(u):
            sl=four(u); w=two(u)
            state(u,wait)
            for d in range(4): o3(u,d).wait_send()
            for g in range(2):
                a,b=AB[g]; p,m=P2[g]
                for d in (p,m): o2(u,d).wait_recv(); o3(u,d).wait_recv()
                for h in range(2):
                    q=2*g+h
                    tot=pf[w,q,b]+(f(q3[sl,p])+f(q2[sl,m]) if h==0 else f(q2[sl,p])+f(q3[sl,m]))
                    gr=f(tot.astype(bf)); cs=slice(q*Q,(q+1)*Q)
                    mn=0.9*min_[w,:,cs]+0.1*gr
                    vn=0.95*vin[w,:,cs]+0.05*gr*gr
                    wo=f(win[w,:,cs])
                    wst[w,q]=(wo-0.02*(mn*lax.rsqrt(vn+1e-8)+0.1*wo)).astype(bf)
                    gst[w,:,cs]=gr.astype(bf)
                for s in range(2): g1(u,g,s).start()
                cp(wst.at[w,pair(g)],wag.at[loc(u),c,pair(g),a,b],csem.at[w,g]).start()
            cp(gst.at[w],gsum.at[loc(u)],nsem.at[w]).start()
        def sB4(u):
            for g,s in GS:
                g1(u,g,s).wait_recv(); g2(u,g,s).start()
        def sB5(u):
            w=rem(u,2)
            for g,s in GS:
                g1(u,g,s).wait_send(); g2(u,g,s).wait_send()
            for g in range(2):
                a,b=AB[g]
                cp(wst.at[w,pair(g)],wag.at[loc(u),c,pair(g),a,b],csem.at[w,g]).wait()
                for s in range(2): g2(u,g,s).wait_recv()
                for s in range(2): g3(u,g,s).start()
            cp(gst.at[w],gsum.at[loc(u)],nsem.at[w]).wait()
        def sB6(u):
            for g,s in GS: g3(u,g,s).wait_send()
            for g,s in GS:
                g3(u,g,s).wait_recv(); g4(u,g,s).start()
        def sB7(u):
            for g,s in GS: g4(u,g,s).wait()
            gd(u).start()
        def sB8(u): gd(u).wait()
        def part(u,h):
            lhs_wait(u,h)
            rsl=jnp.where(jk(u)[0]==3,1,0)
            for q in range(4):
                o=dot(lhs[h].reshape(S*S*R,T),rhs[rsl,:,q*Q:(q+1)*Q]).astype(bf)
                for A in range(S):
                    for B in range(S):
                        blk=o[(A*S+B)*R:(A*S+B+1)*R]
                        o_,i_=(A,B) if q<2 else (B,A)
                        if h: dsend[q,o_,i_]=blk
                        else: own[rem(u,3),q,o_,i_]=blk
            @pl.when(u+1<U)
            def _(): lhs_load(u+1,h)
        tiles=lambda r: pl.ds(pl.multiple_of(r*TM,TM),TM)
        def da_load(v):
            r,h=div(v,2),rem(v,2); rr=tiles(r)
            @pl.when(h==0)
            def _(): cp(du1.at[rr],gt,gsem.at[0]).start()
            @pl.when(h==1)
            def _():
                cp(dg1.at[rr],gt,gsem.at[0]).start()
                cp(h1.at[rr],ht,gsem.at[1]).start(); cp(dy.at[rr],yt,gsem.at[2]).start()
        def w1_load(): return [cp(wu.at[1],wbuf.at[0],wsem.at[0]),cp(wg.at[1],wbuf.at[1],wsem.at[1])]
        def wd_load(): return [cp(wd.at[0,pl.ds(k*Dm,Dm)],wbuf.at[0,:,pl.ds(k*Dm,Dm)],wsem.at[2+k]) for k in range(K)]
        def da_slice(v):
            r,h=div(v,2),rem(v,2); rr=tiles(r)
            @pl.when(v==0)
            def _():
                for d in w1_load(): d.wait()
            cp(du1.at[rr],gt,gsem.at[0]).wait()
            da=dot_nt(gt[...],wbuf[h]).astype(bf)
            @pl.when(h==0)
            def _(): ut[...]=da
            @pl.when(h==1)
            def _():
                cp(h1.at[rr],ht,gsem.at[1]).wait(); cp(dy.at[rr],yt,gsem.at[2]).wait()
                db=f((f(da)+f(ut[...])).astype(bf))
                wide=f(ht[...])
                sc=lax.rsqrt(jnp.mean(wide*wide,-1,keepdims=True)+1e-6)
                dn=db*sc-wide*(sc*sc*sc*jnp.mean(db*wide,-1,keepdims=True))
                rhs[1,rr,:]=(f(yt[...])+f(dn.astype(bf))).astype(bf)
            @pl.when(v<7)
            def _(): da_load(v+1)
            @pl.when(v==7)
            def _():
                for d in wd_load(): d.start()
                for r in (0,1):
                    for d in st_load(0,r): d.start()
        HC=Dm//2
        def st_load(v,r):
            cc=pl.ds(pl.multiple_of(v*HC,HC),HC); rr=pl.ds(r*TM,TM); sl=r%2
            return [cp(s0.at[rr,cc],st.at[sl],ssem.at[0,sl]),cp(t0.at[rr,cc],tt.at[sl],ssem.at[1,sl])]
        def put(v,r):
            cc=pl.ds(pl.multiple_of(v*HC,HC),HC); rr=pl.ds(r*TM,TM)
            return [cp(gt.at[:,pl.ds((2*r+h)*HC,HC)],o.at[rr,cc],osem.at[h,r]) for h,o in enumerate((dg0,du0))]
        def dh_slice(v,rs):
            k=div(v,2); w=wbuf[0,pl.ds(pl.multiple_of(rem(v,2)*HC,HC),HC),pl.ds(pl.multiple_of(k*Dm,Dm),Dm)]
            for r in rs:
                for d in st_load(v,r): d.wait()
                dh=f(dot_nt(rhs[1,r*TM:(r+1)*TM,:],w).astype(bf))
                gt[:,(2*r)*HC:(2*r+1)*HC]=(dh*tt[r%2]).astype(bf)
                gt[:,(2*r+1)*HC:(2*r+2)*HC]=(dh*st[r%2]).astype(bf)
                for d in put(v,r): d.start()
        def dh_first(v):
            @pl.when(v==0)
            def _():
                for d in wd_load(): d.wait()
            @pl.when(v>0)
            def _():
                for r in (2,3):
                    for d in put(v-1,r): d.wait()
            dh_slice(v,(0,1))
            for r in (2,3):
                for d in st_load(v,r): d.start()
        def dh_second(v):
            dh_slice(v,(2,3))
            for r in (0,1):
                for d in put(v,r): d.wait()
            @pl.when(v<2*K-1)
            def _():
                for r in (0,1):
                    for d in st_load(v+1,r): d.start()
            @pl.when(v==2*K-1)
            def _():
                for r in (2,3):
                    for d in put(v,r): d.wait()
        lhs_load(0,1); rhs_load(0); lhs_load(0,0)
        da_load(0)
        for d in w1_load(): d.start()
        @pl.loop(0,N)
        def _(i):
            at(i,4,sA4); at(i,3,sA3); at(i,2,sA2); at(i,1,sA1)
            @pl.when(i<U)
            def _():
                rhs_wait(i)
                part(i,1)
                d2(i).start()
            at(i,3,sB3); at(i,4,sB4); at(i,5,sB5); at(i,6,sB6); at(i,7,sB7); at(i,8,sB8)
            at(i,3,lambda u: state(u,start))
            @pl.when((i>=12)&(i<12+2*K))
            def _(): dh_first(i-12)
            @pl.when(i<U)
            def _():
                part(i,0)
                @pl.when(i+1<U)
                def _(): rhs_load(i+1)
            @pl.when((i>=4)&(i<12))
            def _(): da_slice(i-4)
            @pl.when((i>=12)&(i<12+2*K))
            def _(): dh_second(i-12)
    A=pl.BlockSpec(memory_space=pl.ANY)
    sd=jax.ShapeDtypeStruct
    V=pltpu.VMEM; DS=pltpu.SemaphoreType.DMA
    msg=lambda k: V((k,4,S,R,Q),bf)
    small=lambda k: V((k,4,R,Q),bf)
    out=pl.pallas_call(kern,
        in_specs=[A]*19,out_specs=[A]*4,
        out_shape=[sd((U,2,4,S,S,R,Q),bf)]+[sd((U,R,Dm),bf)]+[sd((T,F),bf)]*2,
        scratch_shapes=[V((2,S,S,R,T),bf),V((2,T,Dm),bf),V((3,4,S,S,R,Q),bf),V((4,S,S,R,Q),bf),V((4,4,S,S,R,Q),bf),
            msg(4),msg(4),msg(4),msg(2),msg(2),msg(2),V((2,4,S,R,Q),f32),
            small(4),small(4),small(4),small(2),small(2),small(2),
            V((2,4,R,Q),bf),V((2,R,Dm),bf),V((2,R,Dm),f32),V((2,R,Dm),f32),V((2,R,Dm),bf),
            V((2,Dm,F),bf),V((TM,F),bf),V((TM,Dm),bf),V((TM,Dm),bf),V((TM,Dm),bf),V((2,TM,Dm//2),f32),V((2,TM,Dm//2),f32),
            DS((2,)),DS(()),DS((2+K,)),DS((3,)),DS((2,2)),DS((2,4)),DS((3,2)),DS((2,)),DS((2,2)),
            DS(()),DS((4,)),DS((10,2,4)),DS((10,4,4)),DS((2,)),DS((4,))],
        compiler_params=pltpu.CompilerParams(collective_id=0,has_side_effects=True,vmem_limit_bytes=67043328),name="mega",
    )(hv(hid1T),av(a1T),hv(hid0T),av(a0T),dy,dg1,du1,wg,wu,wd,s0,t0,h1,mg,mu,md,vg,vu,vd)
    return out

def final(wag,gsum,ms,vs):
    U,_,_,S,_,R,Q=wag.shape; n=2*S*S; Dm=4*Q; L=ms[0].shape[0]; K=U//(3*L)
    ms=(ms[0].reshape(L,K,R,Dm),*ms[1:]); vs=(vs[0].reshape(L,K,R,Dm),*vs[1:])
    B=2
    def kern(w_ref,g_ref,*refs):
        m,v,wo,mo,vo=(refs[3*i:3*i+3] for i in range(5))
        kind=div(B*pl.program_id(0),L*K)
        for t in range(3):
            @pl.when(kind==t)
            def _():
                for p in range(B):
                    for cc in range(2):
                        for r in range(S*S):
                            for q in range(4):
                                v_=w_ref[p,cc,q,r//S,r%S] if q<2 else w_ref[p,cc,q,r%S,r//S]
                                if t: wo[t][0,(2*r+cc)*R:(2*r+cc+1)*R,p*Dm+q*Q:p*Dm+q*Q+Q]=v_
                                else: wo[t][0,2*r+cc,p,:,q*Q:q*Q+Q]=v_
                    g=g_ref[p].astype(f32)
                    at=(0,slice(None),slice(p*Dm,p*Dm+Dm)) if t else (0,p)
                    mo[t][at]=0.9*m[t][at]+0.1*g
                    vo[t][at]=0.95*v[t][at]+0.05*g*g
    H=K//B; E=L*H
    def lk(s,t): s=jnp.clip(s-t*E,0,E-1); return div(s,H),rem(s,H)
    def unit(s): l,k=lk(rem(s,E),0); return ((L-1-l)*3+div(s,E))*H+k
    def spec(t,d,g):
        def at(s): l,k=lk(s,t); return (l,0,k) if t else (l,*[0]*(len(d)-4),k,0,0)
        return pl.BlockSpec(g if t else d,at)
    sd=jax.ShapeDtypeStruct
    mom=[spec(t,(1,B,R,Dm),(1,R,B*Dm)) for t in range(3)]
    o=pl.pallas_call(kern,grid=(U//B,),
        in_specs=[pl.BlockSpec((B,2,4,S,S,R,Q),lambda s:(unit(s),*[0]*6)),pl.BlockSpec((B,R,Dm),lambda s:(unit(s),0,0))]+mom*2,
        out_specs=[spec(t,(1,n,B,R,Dm),(1,Dm,B*Dm)) for t in range(3)]+mom*2,
        out_shape=[sd((L,n,K,R,Dm),bf),sd((L,Dm,K*Dm),bf),sd((L,Dm,K*Dm),bf)]+[sd(a.shape,f32) for a in (*ms,*vs)],
        name="final",compiler_params=pltpu.CompilerParams(vmem_limit_bytes=VM))(wag,gsum,*ms,*vs)
    w,m,v=o[:3],o[3:6],o[6:]
    order=lambda d,g,u: (g,u,d.reshape(L,-1,Dm))
    return (*order(*w),*order(*m),*order(*v))

def solution(mesh):
    from jax.sharding import PartitionSpec as P
    n=mesh.shape["dp"]
    def step(x,dy,wg,wu,wd,mg,mu,md,vg,vu,vd):
        x,dy=x[0],dy[0]
        hid0,hid0T,s0,t0,a0T=p0(x,wg,wu)
        h1,a1,a1T=p1(x,hid0,wd)
        hid1T,dg1,du1=p2(a1,dy,wg,wu,wd,1)
        wag,gsum,_,_=mega(n,hid1T,a1T,hid0T,a0T,dy,dg1,du1,wg,wu,wd,s0,t0,h1,mg,mu,md,vg,vu,vd)
        return final(wag,gsum,(md,mg,mu),(vd,vg,vu))
    tok=P(("rep","dp"),None,None); w=P(None,None,None); m=P(None,"dp",None)
    return jax.shard_map(step,mesh=mesh,in_specs=(tok,tok,w,w,w)+(m,)*6,
        out_specs=(P("rep",None,None),)*3+(P("rep","dp",None),)*6,check_vma=False)
```

time: 1150 us -> 487 us (0.42)
  waiting for transfers between devices: 598 us -> 0 us
  Pallas kernels: 0 us -> 486 us
  matrix products: 398 us -> 0 us
  other arithmetic: 83.5 us -> 0 us
  local copies, waits for them, and re-layouts: 50 us -> 0 us
  between operations: 14.6 us -> 0.81 us
    pallas_call x0 -> x5, Pallas kernels: none -> 486 us  [the longest x1 306 us: mega(): pl.pallas_call(kern, in_specs=[A] * 19, out_specs=[A] * 4, out_shape=[sd(...]
    dot_general x15 -> x0, matrix products: 398 us -> none  [the longest x5 137 us: layer(): gate = jnp.dot(a, w['w_gate'], preferred_element_type=jnp.float32)]
    unnamed x15 -> x0, waiting for transfers between devices: 393 us -> none
    reshape x3 -> x0, waiting for transfers between devices: 205 us -> none  [step(): t.reshape(-1, *t.shape[2:])]
    unnamed x4 -> x0, other arithmetic: 63.6 us -> none
    unnamed x43 -> x0, local copies, waits for them, and re-layouts: 50 us -> none
  transfers between devices with their start and end apart: 9 -> 0, of which waited for: 7 -> 0; matrix products, arithmetic and copies ran while one was open for 27% -> 0% of each run, Pallas kernels for 0% -> 0%
where the time goes in v1:
time: 487 us
  Pallas kernels  486 us (100%)
    pallas_call x1, Pallas kernels, mega(): pl.pallas_call(kern, in_specs=[A] * 19, out_specs=[A] * 4, out_shape=[sd(...  306 us
    pallas_call x1, Pallas kernels, p2(): pl.pallas_call(kern, grid=(F // tf, T // tm), in_specs=[pl.BlockSpec((T,...  64.6 us
    pallas_call x1, Pallas kernels, p0(): pl.pallas_call(kern, grid=(F // tf, nt), in_specs=[pl.BlockSpec((tm, Dm),...  51.9 us
    pallas_call x1, Pallas kernels, final(): pl.pallas_call(kern, grid=(U // B,), in_specs=[pl.BlockSpec((B, 2, 4, S,...  37 us
    pallas_call x1, Pallas kernels, p1(): pl.pallas_call(kern, grid=(T // tm,), in_specs=[pl.BlockSpec((tm, Dm), la...  26 us

profile of v1, /device:TPU:97, one launch (start us, length us, event | category | flops | bytes accessed | tf_op | source)
XLA Modules:
  0.0 486.9 jit_solution(8837123931335981414)
XLA Ops:
  0.6 51.9 %p0.1 = (bf16[2048,4096]{1,0:T(8,128)(2,1)}, bf16[4096,2048]{1,0:T(8,128)(2,1)}, f32[2048,4096]{1,0:T(8,128)}, f32[2048,4096]{1,0:T(8,128)}, bf16[1024,2048]{1,0:T(8,128)(2,1)}) custom-call(bf16[2048,1024]{1,0:T(8,128)(2,1)} %bitcast.15, bf16[2,1024,4096]{2,1,0:T(8,128)(2,1)} %wg.1, bf16[2,1024,4096]{2,1,0:T(8,128)(2,1)} %wu.1), custom_call_target="tpu_custom_call" | custom-call | tf_op jit(solution)/shard_map/p0/pallas_call | solution.py:35
  52.6 26.0 %p1.1 = (bf16[2048,1024]{1,0:T(8,128)(2,1)}, bf16[2048,1024]{1,0:T(8,128)(2,1)}, bf16[1024,2048]{1,0:T(8,128)(2,1)}) custom-call(bf16[2048,1024]{1,0:T(8,128)(2,1)} %bitcast.16, bf16[2048,4096]{1,0:T(8,128)(2,1)} %get-tuple-element.31.hid_ref, bf16[2,4096,1024]{2,1,0:T(8,128)(2,1)} %wd.1), custom_call_target="tpu_custom_call" | custom-call | tf_op jit(solution)/shard_map/p1/pallas_call | solution.py:56
  78.6 64.6 %p2.1 = (bf16[4096,2048]{1,0:T(8,128)(2,1)}, bf16[2048,4096]{1,0:T(8,128)(2,1)}, bf16[2048,4096]{1,0:T(8,128)(2,1)}) custom-call(bf16[2048,1024]{1,0:T(8,128)(2,1)} %get-tuple-element.32.a_ref, bf16[2048,1024]{1,0:T(8,128)(2,1)} %bitcast.11, bf16[2,1024,4096]{2,1,0:T(8,128)(2,1)} %wg.1, bf16[2,1024,4096]{2,1,0:T(8,128)(2,1)} %wu.1, bf16[2,4096,1024]{2,1,0:T(8,128)(2,1)} %wd.1), custom_call_target="tpu_custom_call" | custom-call | tf_op jit(solution)/shard_map/p2/pallas_call | solution.py:77
  143.2 306.5 %mega.1 = (bf16[24,2,4,4,4,32,256]{6,5,4,3,2,1,0:T(8,128)(2,1)}, bf16[24,32,1024]{2,1,0:T(8,128)(2,1)}, bf16[2048,4096]{1,0:T(8,128)(2,1)}, bf16[2048,4096]{1,0:T(8,128)(2,1)}) custom-call(bf16[4,4,2,4,32,2048]{5,4,3,2,1,0:T(8,128)(2,1)} %bitcast.14, bf16[4,4,2,32,2048]{4,3,2,1,0:T(8,128)(2,1)} %bitcast.20, bf16[4,4,2,4,32,2048]{5,4,3,2,1,0:T(8,128)(2,1)} %bitcast.13, ...), custom_call_target="tpu_custom_call" | custom-call | tf_op jit(solution)/shard_map/mega/pallas_call | solution.py:388
  449.7 37.0 %final.1 = (bf16[2,32,4,32,1024]{4,3,2,1,0:T(8,128)(2,1)}, bf16[2,1024,4096]{2,1,0:T(8,128)(2,1)}, bf16[2,1024,4096]{2,1,0:T(8,128)(2,1)}, f32[2,4,32,1024]{3,2,...) custom-call(bf16[24,2,4,4,4,32,256]{6,5,4,3,2,1,0:T(8,128)(2,1)} %ge, ...), custom_call_target="tpu_custom_call" | custom-call | tf_op jit(solution)/shard_map/final/pallas_call | solution.py:431

commit v2 on v1

--- a/solution.py
+++ b/solution.py
@@ -11,53 +11,54 @@
     wide=h.astype(f32)
     return (wide*lax.rsqrt(jnp.mean(wide**2,-1,keepdims=True)+1e-6)).astype(bf)
 
-def p0(x,wg,wu,tm=1024,tf=512,rm=256,rf=256):
-    T,Dm=x.shape; F=wg.shape[-1]
-    def kern(x_ref,wg_ref,wu_ref,hid_ref,hidT_ref,s_ref,t_ref,aT_ref,a_sc):
-        f=pl.program_id(0); t=pl.program_id(1)
+def p01(x,wg,wu,wd,tm=512,tf=1024,rm=256,rf=256):
+    T,Dm=x.shape; F=wg.shape[-1]; nf=F//tf
+    def kern(x_ref,wg,wu,wd,hidT_ref,s_ref,t_ref,aT_ref,h_ref,a_ref,a1T_ref,gs,us,ds,a_sc,hid_sc,acc,sem):
+        t,f=pl.program_id(0),pl.program_id(1)
+        part=lambda f: pl.ds(pl.multiple_of(f*tf,tf),tf)
+        def loads(f):
+            p=part(f)
+            return [pltpu.make_async_copy(a,b,sem.at[i,f]) for i,(a,b) in enumerate(((wg.at[0,:,p],gs.at[:,p]),(wu.at[0,:,p],us.at[:,p]),(wd.at[0,p],ds.at[p])))]
+        @pl.when((t==0)&(f==0))
+        def _():
+            for g in range(nf):
+                for d in loads(g): d.start()
         @pl.when(f==0)
         def _():
             a=normed(x_ref[...])
-            a_sc[pl.ds(pl.multiple_of(t*tm,tm),tm),:]=a
+            a_sc[...]=a
             aT_ref[...]=a.T
+            acc[...]=jnp.zeros_like(acc)
+        @pl.when(t==0)
+        def _():
+            for d in loads(f): d.wait()
         for r in range(tm//rm):
-            a=a_sc[pl.ds(pl.multiple_of(t*tm+r*rm,rm),rm),:]
+            rs=slice(r*rm,(r+1)*rm); a=a_sc[rs,:]
             for c in range(tf//rf):
-                cs=slice(c*rf,(c+1)*rf); rs=slice(r*rm,(r+1)*rm)
-                gate=dot(a,wg_ref[0,:,cs]); up=dot(a,wu_ref[0,:,cs])
+                cs=slice(c*rf,(c+1)*rf); cols=pl.ds(pl.multiple_of(f*tf+c*rf,rf),rf)
+                gate=dot(a,gs[:,cols]); up=dot(a,us[:,cols])
                 sg=jax.nn.sigmoid(gate); s=gate*sg
                 s_ref[rs,cs]=s
                 t_ref[rs,cs]=up*(sg*(1.0+gate*(1.0-sg)))
                 hid=(s*up).astype(bf)
-                hid_ref[rs,cs]=hid
+                hid_sc[rs,cs]=hid
                 hidT_ref[cs,rs]=hid.T
-    nt=T//tm; last=nt-1
-    return pl.pallas_call(kern,grid=(F//tf,nt),
-        in_specs=[pl.BlockSpec((tm,Dm),lambda f,t:(jnp.where(f==0,t,last),0)),
-                  pl.BlockSpec((1,Dm,tf),lambda f,t:(0,0,f)),pl.BlockSpec((1,Dm,tf),lambda f,t:(0,0,f))],
-        out_specs=[pl.BlockSpec((tm,tf),lambda f,t:(t,f)),pl.BlockSpec((tf,tm),lambda f,t:(f,t)),
-                   pl.BlockSpec((tm,tf),lambda f,t:(t,f)),pl.BlockSpec((tm,tf),lambda f,t:(t,f)),
-                   pl.BlockSpec((Dm,tm),lambda f,t:(0,jnp.where(f==0,t,last)))],
-        out_shape=[jax.ShapeDtypeStruct((T,F),bf),jax.ShapeDtypeStruct((F,T),bf),jax.ShapeDtypeStruct((T,F),f32),jax.ShapeDtypeStruct((T,F),f32),jax.ShapeDtypeStruct((Dm,T),bf)],
-        scratch_shapes=[pltpu.VMEM((T,Dm),bf)],
-        compiler_params=pltpu.CompilerParams(vmem_limit_bytes=VM,dimension_semantics=("arbitrary","arbitrary")),name="p0")(x,wg,wu)
-
-def p1(x,hid,wd,tm=512):
-    T,Dm=x.shape; F=hid.shape[1]
-    def kern(x_ref,hid_ref,wd_ref,h_ref,a_ref,aT_ref):
-        for r in range(tm//256):
-            rs=slice(r*256,(r+1)*256)
-            y=dot(hid_ref[rs,:],wd_ref[0]).astype(bf)
-            h=x_ref[rs,:]+y
-            h_ref[rs,:]=h
+        acc[...]+=dot(hid_sc[...],ds[part(f),:])
+        @pl.when(f==nf-1)
+        def _():
+            h=x_ref[...]+acc[...].astype(bf)
+            h_ref[...]=h
             a=normed(h)
-            a_ref[rs,:]=a
-            aT_ref[:,rs]=a.T
-    return pl.pallas_call(kern,grid=(T//tm,),
-        in_specs=[pl.BlockSpec((tm,Dm),lambda t:(t,0)),pl.BlockSpec((tm,F),lambda t:(t,0)),pl.BlockSpec((1,F,Dm),lambda t:(0,0,0))],
-        out_specs=[pl.BlockSpec((tm,Dm),lambda t:(t,0)),pl.BlockSpec((tm,Dm),lambda t:(t,0)),pl.BlockSpec((Dm,tm),lambda t:(0,t))],
-        out_shape=[jax.ShapeDtypeStruct((T,Dm),bf),jax.ShapeDtypeStruct((T,Dm),bf),jax.ShapeDtypeStruct((Dm,T),bf)],
-        compiler_params=pltpu.CompilerParams(vmem_limit_bytes=VM),name="p1")(x,hid,wd)
+            a_ref[...]=a
+            a1T_ref[...]=a.T
+    A=pl.BlockSpec(memory_space=pl.ANY)
+    row=pl.BlockSpec((tm,Dm),lambda t,f:(t,0)); col=pl.BlockSpec((Dm,tm),lambda t,f:(0,t)); tile=pl.BlockSpec((tm,tf),lambda t,f:(t,f))
+    sd=jax.ShapeDtypeStruct; V=pltpu.VMEM
+    return pl.pallas_call(kern,grid=(T//tm,nf),in_specs=[row,A,A,A],
+        out_specs=[pl.BlockSpec((tf,tm),lambda t,f:(f,t)),tile,tile,col,row,row,col],
+        out_shape=[sd((F,T),bf),sd((T,F),f32),sd((T,F),f32),sd((Dm,T),bf),sd((T,Dm),bf),sd((T,Dm),bf),sd((Dm,T),bf)],
+        scratch_shapes=[V((Dm,F),bf),V((Dm,F),bf),V((F,Dm),bf),V((tm,Dm),bf),V((tm,tf),bf),V((tm,Dm),f32),pltpu.SemaphoreType.DMA((3,nf))],
+        compiler_params=pltpu.CompilerParams(vmem_limit_bytes=VM),name="p01")(x,wg,wu,wd)
 
 def p2(a,dy,wg,wu,wd,layer,tm=1024,tf=512,rm=256,rf=256):
     T,Dm=a.shape; F=wg.shape[-1]
@@ -101,10 +102,6 @@
         c=rem(me,2); y=rem(div(me,2),S); x=div(me,2*S)
         idx=lambda x,y,c: (rem(x+S,S)*S+rem(y+S,S))*2+c
         nb=[idx(x+1,y,c),idx(x-1,y,c),idx(x,y+1,c),idx(x,y-1,c)]; pa=idx(x,y,1-c)
-        bar=pltpu.get_barrier_semaphore()
-        for d in nb+[pa]:
-            pl.semaphore_signal(bar,inc=1,device_id={axis:d},device_id_type=MESH)
-        pl.semaphore_wait(bar,5)
         AB=[(x,y),(y,x)]
         P1=[(0,1),(2,3)]; P2=[(2,3),(0,1)]
         def rc(src,dst,s,r,dev):
@@ -357,6 +354,10 @@
                 for r in (2,3):
                     for d in put(v,r): d.wait()
         lhs_load(0,1); rhs_load(0); lhs_load(0,0)
+        bar=pltpu.get_barrier_semaphore()
+        for d in nb+[pa]:
+            pl.semaphore_signal(bar,inc=1,device_id={axis:d},device_id_type=MESH)
+        pl.semaphore_wait(bar,5)
         da_load(0)
         for d in w1_load(): d.start()
         @pl.loop(0,N)
@@ -442,8 +443,7 @@
     n=mesh.shape["dp"]
     def step(x,dy,wg,wu,wd,mg,mu,md,vg,vu,vd):
         x,dy=x[0],dy[0]
-        hid0,hid0T,s0,t0,a0T=p0(x,wg,wu)
-        h1,a1,a1T=p1(x,hid0,wd)
+        hid0T,s0,t0,a0T,h1,a1,a1T=p01(x,wg,wu,wd)
         hid1T,dg1,du1=p2(a1,dy,wg,wu,wd,1)
         wag,gsum,_,_=mega(n,hid1T,a1T,hid0T,a0T,dy,dg1,du1,wg,wu,wd,s0,t0,h1,mg,mu,md,vg,vu,vd)
         return final(wag,gsum,(md,mg,mu),(vd,vg,vu))

time: 487 us -> 480 us (0.986)
  Pallas kernels: 486 us -> 479 us
    pallas_call x2 -> x1, Pallas kernels: 78 us -> 73.9 us  [p01(): pl.pallas_call(kern, grid=(T // tm, nf), in_specs=[row, A, A, A], out_spe...]
where the time goes in v2:
time: 480 us
  Pallas kernels  479 us (100%)
    pallas_call x1, Pallas kernels, mega(): pl.pallas_call(kern, in_specs=[A] * 19, out_specs=[A] * 4, out_shape=[sd(...  304 us
    pallas_call x1, Pallas kernels, p01(): pl.pallas_call(kern, grid=(T // tm, nf), in_specs=[row, A, A, A], out_spe...  73.9 us
    pallas_call x1, Pallas kernels, p2(): pl.pallas_call(kern, grid=(F // tf, T // tm), in_specs=[pl.BlockSpec((T,...  64.7 us
    pallas_call x1, Pallas kernels, final(): pl.pallas_call(kern, grid=(U // B,), in_specs=[pl.BlockSpec((B, 2, 4, S,...  37 us

profile of v2, /device:TPU:97, one launch (start us, length us, event | category | flops | bytes accessed | tf_op | source)
XLA Modules:
  0.0 480.1 jit_solution(8409991848318775997)
XLA Ops:
  0.6 73.9 %p01.1 = (bf16[4096,2048]{1,0:T(8,128)(2,1)}, f32[2048,4096]{1,0:T(8,128)}, f32[2048,4096]{1,0:T(8,128)}, bf16[1024,2048]{1,0:T(8,128)(2,1)}, bf16[2048,1024]{1,...) custom-call(bf16[2048,1024]{1,0:T(8,128)(2,1)} %bitcast.19, bf16[2,1024,4096]{2,1,0:T(8,128)(2,1)} %wg.3, ...), custom_call_target="tpu_custom_call" | custom-call | tf_op jit(solution)/shard_map/p01/pallas_call | solution.py:57
  74.5 64.7 %p2.1 = (bf16[4096,2048]{1,0:T(8,128)(2,1)}, bf16[2048,4096]{1,0:T(8,128)(2,1)}, bf16[2048,4096]{1,0:T(8,128)(2,1)}) custom-call(bf16[2048,1024]{1,0:T(8,128)(2,1)} %get-tuple-element.30.a_ref, bf16[2048,1024]{1,0:T(8,128)(2,1)} %bitcast.11, bf16[2,1024,4096]{2,1,0:T(8,128)(2,1)} %wg.3, bf16[2,1024,4096]{2,1,0:T(8,128)(2,1)} %wu.3, bf16[2,4096,1024]{2,1,0:T(8,128)(2,1)} %wd.3), custom_call_target="tpu_custom_call" | custom-call | tf_op jit(solution)/shard_map/p2/pallas_call | solution.py:78
  139.2 303.8 %mega.1 = (bf16[24,2,4,4,4,32,256]{6,5,4,3,2,1,0:T(8,128)(2,1)}, bf16[24,32,1024]{2,1,0:T(8,128)(2,1)}, bf16[2048,4096]{1,0:T(8,128)(2,1)}, bf16[2048,4096]{1,0:T(8,128)(2,1)}) custom-call(bf16[4,4,2,4,32,2048]{5,4,3,2,1,0:T(8,128)(2,1)} %bitcast.14, bf16[4,4,2,32,2048]{4,3,2,1,0:T(8,128)(2,1)} %bitcast.18, bf16[4,4,2,4,32,2048]{5,4,3,2,1,0:T(8,128)(2,1)} %bitcast.13, ...), custom_call_target="tpu_custom_call" | custom-call | tf_op jit(solution)/shard_map/mega/pallas_call | solution.py:389
  443.0 37.0 %final.1 = (bf16[2,32,4,32,1024]{4,3,2,1,0:T(8,128)(2,1)}, bf16[2,1024,4096]{2,1,0:T(8,128)(2,1)}, bf16[2,1024,4096]{2,1,0:T(8,128)(2,1)}, f32[2,4,32,1024]{3,2,...) custom-call(bf16[24,2,4,4,4,32,256]{6,5,4,3,2,1,0:T(8,128)(2,1)} %ge, ...), custom_call_target="tpu_custom_call" | custom-call | tf_op jit(solution)/shard_map/final/pallas_call | solution.py:432

commit v3 on v2

--- a/solution.py
+++ b/solution.py
@@ -65,7 +65,7 @@
     def kern(a_ref,dy_ref,wg_ref,wu_ref,wd_ref,hidT_ref,dg_ref,du_ref):
         t=pl.program_id(1)
         for r in range(tm//rm):
-            ro=pl.ds(pl.multiple_of(t*tm+r*rm,rm),rm)
+            ro=slice(r*rm,(r+1)*rm)
             av=a_ref[ro,:]; dv=dy_ref[ro,:]
             for c in range(tf//rf):
                 cs=slice(c*rf,(c+1)*rf); rs=slice(r*rm,(r+1)*rm)
@@ -76,7 +76,7 @@
                 dg_ref[rs,cs]=(dh*(up*(sg*(1.0+gate*(1.0-sg))))).astype(bf)
                 hidT_ref[cs,rs]=(s*up).astype(bf).T
     return pl.pallas_call(kern,grid=(F//tf,T//tm),
-        in_specs=[pl.BlockSpec((T,Dm),lambda f,t:(0,0)),pl.BlockSpec((T,Dm),lambda f,t:(0,0)),
+        in_specs=[pl.BlockSpec((tm,Dm),lambda f,t:(t,0)),pl.BlockSpec((tm,Dm),lambda f,t:(t,0)),
                   pl.BlockSpec((1,Dm,tf),lambda f,t:(layer,0,f)),pl.BlockSpec((1,Dm,tf),lambda f,t:(layer,0,f)),pl.BlockSpec((1,tf,Dm),lambda f,t:(layer,f,0))],
         out_specs=[pl.BlockSpec((tf,tm),lambda f,t:(f,t)),pl.BlockSpec((tm,tf),lambda f,t:(t,f)),pl.BlockSpec((tm,tf),lambda f,t:(t,f))],
         out_shape=[jax.ShapeDtypeStruct((F,T),bf),jax.ShapeDtypeStruct((T,F),bf),jax.ShapeDtypeStruct((T,F),bf)],

time: 480 us -> 483 us (level)
  no operation moved by 1% of the time
where the time goes in v3:
time: 483 us
  Pallas kernels  482 us (100%)
    pallas_call x1, Pallas kernels, mega(): pl.pallas_call(kern, in_specs=[A] * 19, out_specs=[A] * 4, out_shape=[sd(...  304 us
    pallas_call x1, Pallas kernels, p01(): pl.pallas_call(kern, grid=(T // tm, nf), in_specs=[row, A, A, A], out_spe...  73.9 us
    pallas_call x1, Pallas kernels, p2(): pl.pallas_call(kern, grid=(F // tf, T // tm), in_specs=[pl.BlockSpec((tm,...  67.1 us
    pallas_call x1, Pallas kernels, final(): pl.pallas_call(kern, grid=(U // B,), in_specs=[pl.BlockSpec((B, 2, 4, S,...  37 us

profile of v3, /device:TPU:97, one launch (start us, length us, event | category | flops | bytes accessed | tf_op | source)
XLA Modules:
  0.0 482.6 jit_solution(9056082663568624415)
XLA Ops:
  0.6 73.9 %p01.1 = (bf16[4096,2048]{1,0:T(8,128)(2,1)}, f32[2048,4096]{1,0:T(8,128)}, f32[2048,4096]{1,0:T(8,128)}, bf16[1024,2048]{1,0:T(8,128)(2,1)}, bf16[2048,1024]{1,...) custom-call(bf16[2048,1024]{1,0:T(8,128)(2,1)} %bitcast.19, bf16[2,1024,4096]{2,1,0:T(8,128)(2,1)} %wg.3, ...), custom_call_target="tpu_custom_call" | custom-call | tf_op jit(solution)/shard_map/p01/pallas_call | solution.py:57
  74.5 67.1 %p2.1 = (bf16[4096,2048]{1,0:T(8,128)(2,1)}, bf16[2048,4096]{1,0:T(8,128)(2,1)}, bf16[2048,4096]{1,0:T(8,128)(2,1)}) custom-call(bf16[2048,1024]{1,0:T(8,128)(2,1)} %get-tuple-element.30.a_ref, bf16[2048,1024]{1,0:T(8,128)(2,1)} %bitcast.11, bf16[2,1024,4096]{2,1,0:T(8,128)(2,1)} %wg.3, bf16[2,1024,4096]{2,1,0:T(8,128)(2,1)} %wu.3, bf16[2,4096,1024]{2,1,0:T(8,128)(2,1)} %wd.3), custom_call_target="tpu_custom_call" | custom-call | tf_op jit(solution)/shard_map/p2/pallas_call | solution.py:78
  141.7 303.8 %mega.1 = (bf16[24,2,4,4,4,32,256]{6,5,4,3,2,1,0:T(8,128)(2,1)}, bf16[24,32,1024]{2,1,0:T(8,128)(2,1)}, bf16[2048,4096]{1,0:T(8,128)(2,1)}, bf16[2048,4096]{1,0:T(8,128)(2,1)}) custom-call(bf16[4,4,2,4,32,2048]{5,4,3,2,1,0:T(8,128)(2,1)} %bitcast.14, bf16[4,4,2,32,2048]{4,3,2,1,0:T(8,128)(2,1)} %bitcast.18, bf16[4,4,2,4,32,2048]{5,4,3,2,1,0:T(8,128)(2,1)} %bitcast.13, ...), custom_call_target="tpu_custom_call" | custom-call | tf_op jit(solution)/shard_map/mega/pallas_call | solution.py:389
  445.4 37.0 %final.1 = (bf16[2,32,4,32,1024]{4,3,2,1,0:T(8,128)(2,1)}, bf16[2,1024,4096]{2,1,0:T(8,128)(2,1)}, bf16[2,1024,4096]{2,1,0:T(8,128)(2,1)}, f32[2,4,32,1024]{3,2,...) custom-call(bf16[24,2,4,4,4,32,256]{6,5,4,3,2,1,0:T(8,128)(2,1)} %ge, ...), custom_call_target="tpu_custom_call" | custom-call | tf_op jit(solution)/shard_map/final/pallas_call | solution.py:432
